TPU v7x, 32 devices: a whole 2x2x4 slice. The times are simulated.
32 devices in a mesh: gx: 4 (over y, core), gy: 2 (over x), var: 4 (over z).
Axes of the slice: x: 2, y: 2, z: 4, core: 2. Of those that a mesh axis runs over, the one named last changes fastest.
Arguments:
- field: float32 [4, 32, 256, 256], P('var', None, 'gx', 'gy'), may hold values from -12 to 12
- drive: float32 [4, 32, 40, 40], P('var'), may hold values from -1 to 1
- keep_count: int32 [32], replicated, may hold values from 20 to 79, as said below
- level_class: int32 [32], replicated, may hold values from 0 to 7
- height_table: float32 [8], replicated, may hold values from 0.2 to 1
Outputs:
- nudged: float32 [4, 32, 256, 256], P('var', None, 'gx', 'gy')
Inputs may be any that keep to these rules, and one draw needn't show every extreme that they name: `keep_count`: some level in every draw has the count 2 * 40 - 1, which keeps all 40 x 40 modes.
All inputs are finite; a program needn't handle non-finite values.
Results may differ from a plain program's by a relative error of at most 0.0001.
Values sent between devices are 32-bit elements; how exact they have to be, the bound alone decides.
No kernel may reach another device: no remote copies, remote signals or barrier semaphores. Data moves between devices by JAX's collectives and lax.ppermute only.
A program may use at most 64 MiB of HBM per device.

v0:
```python
import math
import jax
import jax.numpy as jnp
from jax import lax
from jax.sharding import PartitionSpec as P

NVAR = 4
KM = 40
HTAB = 8
energy_weights = (1.0, 1.0, 2.0, 3.0)
strength_top = 0.5
epsilon = 1e-06


def cosine_table(first, count, total, modes):
    cells = first + jnp.arange(count, dtype=jnp.int32)
    waves = jnp.arange(modes, dtype=jnp.int32)
    phase = waves[None, :] * (2 * cells[:, None] + 1) % (4 * total)
    values = jnp.cos(jnp.pi * phase.astype(jnp.float32) / (2.0 * total))
    factor = jnp.where(waves == 0, 1.0, math.sqrt(2.0)).astype(jnp.float32)
    return values * factor[None, :]


def settle(coeff, drive_block, mask, weight):
    delta = mask * (drive_block - coeff)
    gap = weight * jnp.sum(delta * delta)
    model = weight * jnp.sum(mask * coeff * coeff)
    gap, model = lax.psum((gap, model), "var")
    return (delta, gap, model)


def per_device(field, drive, keep_count, level_class, height_table):
    high = lax.Precision.HIGHEST
    block = field[0]
    drive_block = drive[0]
    levels, rows, columns = block.shape
    total_x = rows * lax.axis_size("gx")
    total_y = columns * lax.axis_size("gy")
    table_x = cosine_table(lax.axis_index("gx") * rows, rows, total_x, KM)
    table_y = cosine_table(lax.axis_index("gy") * columns, columns, total_y, KM)
    waves = jnp.arange(KM, dtype=jnp.int32)
    mask = ((waves[:, None] + waves[None, :])[None, :, :] < keep_count[:, None, None]).astype(
        jnp.float32
    )
    onehot = (level_class[:, None] == jnp.arange(HTAB, dtype=jnp.int32)[None, :]).astype(
        jnp.float32
    )
    lift = jnp.dot(onehot, height_table, precision=high)
    variable = lax.axis_index("var")
    weight = jnp.sum(
        jnp.where(
            jnp.arange(NVAR, dtype=jnp.int32) == variable,
            jnp.array(energy_weights, jnp.float32),
            0.0,
        )
    )
    half = jnp.einsum("lij,im->lmj", block, table_x, precision=high)
    partial_value = jnp.einsum("lmj,jn->lmn", half, table_y, precision=high) / float(
        total_x * total_y
    )
    flat = partial_value.reshape(-1)
    summed = lax.psum(flat, ("gx", "gy"))
    delta, gap, model = settle(summed.reshape(levels, KM, KM), drive_block, mask, weight)
    strength = strength_top * gap / (gap + model + epsilon)
    back = jnp.einsum("lmn,jn->lmj", delta, table_y, precision=high)
    increment = jnp.einsum("lmj,im->lij", back, table_x, precision=high)
    nudged = block + strength * lift[:, None, None] * increment
    return nudged[None]


def solution(mesh):
    return jax.shard_map(
        per_device,
        mesh=mesh,
        in_specs=(P("var", None, "gx", "gy"), P("var", None, None, None), P(), P(), P()),
        out_specs=P("var", None, "gx", "gy"),
        check_vma=False,
    )
```

profile of v0, /device:TPU:0, one launch (start us, length us, event | category | flops | bytes accessed | tf_op | source)
XLA Modules:
  0.0 97.3 jit_solution(9964165065591714958)
XLA Ops:
  6.5 0.0 copy-start
  6.5 0.0 all-reduce.3.cloned.1.call-start
  6.6 2.0 %convolution_bitcast_fusion = f32[32,40,128]{2,1,0:T(8,128)S(1)} fusion(f32[1,32,64,128]{3,2,1,0:T(8,128)} %param.6, f32[40]{0:T(128)S(1)} %compare_select_fusion, s32[64]{0:T(128)S(1)} %multiply_add_fusion.1), kind=kOutput, calls=%fused_computation.5 | convolution fusion | flops 125867520 | bytes 1704352 | tf_op jit(solution)/shard_map/lij,im->lmj/dot_general | solution.py:57
  8.6 0.7 convolution_multiply_fusion.1
  9.3 1.1 %reshape.46 = f32[51200]{0:T(1024)} reshape(f32[32,40,40]{2,1,0:T(8,128)S(1)} %convolution_multiply_fusion.1) | data formatting | bytes 409600 | tf_op jit(solution)/shard_map/reshape | solution.py:61
  10.5 0.0 all-reduce.3.cloned.1.call-update
  10.5 0.0 copy-start.3
  10.5 0.6 copy-done.3
  11.2 0.0 copy-start.5
  11.2 0.2 broadcast_compare_fusion
  11.3 0.0 copy-start.2
  11.3 0.5 lt.34
  11.9 0.0 copy-done.5
  11.9 0.6 fusion.56
  12.5 53.3 %all-reduce.3.cloned.1.call-done = f32[51200]{0:T(1024)} async-done(((f32[51200]{0:T(1024)}), f32[51200]{0:T(1024)}) %all-reduce.3.cloned.1.call-update) | async-done | bytes 204816 | tf_op jit(solution)/shard_map/psum | solution.py:62
  65.8 1.6 %fusion.6 = f32[]{:T(128)} fusion(f32[51200]{0:T(1024)} %all-reduce.3.cloned.1.call-done, pred[51200]{0:T(1024)(128)(4,1)S(1)} %lt.34), kind=kLoop, calls=%fused_computation.14 | loop fusion | flops 153599 | bytes 256004 | tf_op jit(solution)/shard_map/reduce_sum | solution.py:27
  68.7 1.4 %reshape.47 = f32[32,40,40]{2,1,0:T(8,128)S(1)} reshape(f32[51200]{0:T(1024)} %all-reduce.3.cloned.1.call-done) | data formatting | bytes 409600 | tf_op jit(solution)/shard_map/reshape | solution.py:63
  70.1 0.0 copy-done.2
  70.1 1.0 multiply_reduce_fusion
  71.0 0.0 copy-start.1
  72.4 0.8 fusion.7
  73.2 12.3 %all-reduce = (f32[]{:T(128)}, f32[]{:T(128)}) all-reduce(f32[]{:T(128)S(6)} %mul.129, f32[]{:T(128)S(6)} %mul.132), channel_id=1, replica_groups=mesh['gx'=4,'gy'=2,'var'=4] {'var'}, use_global_device_ids=true, to_apply=%region_3.4 | all-reduce | flops 2 | bytes 16 | tf_op jit(solution)/shard_map/psum | solution.py:28
  87.5 0.0 copy-start.4
  87.5 0.0 copy-done
  87.5 0.6 copy-done.4
  88.1 0.2 fusion.3
  88.3 0.0 copy-done.1
  88.3 2.2 %fusion.2 = f32[1,32,64,128]{3,2,1,0:T(8,128)} fusion(f32[32,40,128]{2,1,0:T(8,128)S(1)} %fusion.7, f32[1,32,64,128]{3,2,1,0:T(8,128)S(1)} %copy-done.1, f32[32]{0:T(128)S(1)} %fusion.3, f32[40]{0:T(128)S(1)} %compare_select_fusion, s32[64]{0:T(128)S(1)} %multiply_add_fusion.1), kind=kOutput, calls=%fused_computation.3 | convolution fusion | flops 126391808 | bytes 2753056 | tf_op jit(solution)/shard_map/lmj,im->lij/dot_general | solution.py:66
  (4 shorter events, 0.0 us)
Async XLA Ops:
  6.5 81.0 %copy-start = (f32[8]{0:T(128)S(1)}, f32[8]{0:T(128)}, u32[]{:S(2)}) copy-start(f32[8]{0:T(128)} %param.10) | copy-start | bytes 100
  6.5 59.2 %all-reduce.3.cloned.1.call-start = ((), (), s32[]{:S(2)}) async-start(), calls=%async_computation | async-start | bytes 409600 | tf_op jit(solution)/shard_map/psum | solution.py:62
  10.5 0.7 copy-start.3
  11.2 0.7 copy-start.5
  11.3 58.7 %copy-start.2 = (f32[1,32,40,40]{3,2,1,0:T(8,128)S(1)}, f32[1,32,40,40]{3,2,1,0:T(8,128)}, u32[]{:S(2)}) copy-start(f32[1,32,40,40]{3,2,1,0:T(8,128)} %param.7) | copy-start | bytes 614404
  71.0 17.3 %copy-start.1 = (f32[1,32,64,128]{3,2,1,0:T(8,128)S(1)}, f32[1,32,64,128]{3,2,1,0:T(8,128)}, u32[]{:S(2)}) copy-start(f32[1,32,64,128]{3,2,1,0:T(8,128)} %param.6) | copy-start | bytes 3145732
  87.5 0.7 copy-start.4
Sparse Core Ops, SparseCore 0:
  10.6 55.1 all-reduce.2
where the time goes:
time: 97.6 us; the launch traced here: 97.3 us
  waiting for transfers between devices  53.3 us (55%)
  between operations  18.2 us (19%)
  blocking collectives  12.3 us (13%)
  matrix products  5.85 us (6%)
  local copies, waits for them, and re-layouts  4.31 us (4%)
  other arithmetic  3.37 us (3%)
    psum x1, waiting for transfers between devices, per_device(): summed = lax.psum(flat, ('gx', 'gy'))  53.3 us
    psum x1, blocking collectives, settle(): gap, model = lax.psum((gap, model), 'var')  12.3 us
    dot_general x1, matrix products, per_device(): increment = jnp.einsum('lmj,im->lij', back, table_x, precision=high)  2.15 us
    dot_general x1, matrix products, per_device(): half = jnp.einsum('lij,im->lmj', block, table_x, precision=high)  2 us
  transfers between devices with their start and end apart: 1, of which 1 were waited for; matrix products, arithmetic and copies ran while one was open for 1% of the time, Pallas kernels for 0%

commit v1 on v0

--- a/solution.py
+++ b/solution.py
@@ -59,7 +59,7 @@
         total_x * total_y
     )
     flat = partial_value.reshape(-1)
-    summed = lax.psum(flat, ("gx", "gy"))
+    summed = jnp.sum(lax.all_gather(flat, ("gx", "gy")), axis=0)
     delta, gap, model = settle(summed.reshape(levels, KM, KM), drive_block, mask, weight)
     strength = strength_top * gap / (gap + model + epsilon)
     back = jnp.einsum("lmn,jn->lmj", delta, table_y, precision=high)

time: 97.6 us -> 70.5 us (0.72)
  waiting for transfers between devices: 53.3 us -> 28.1 us
  local copies, waits for them, and re-layouts: 4.31 us -> 1.73 us
    psum x1 -> x0, waiting for transfers between devices: 53.3 us -> none  [per_device(): summed = lax.psum(flat, ('gx', 'gy'))]
    all_gather x0 -> x1, waiting for transfers between devices: none -> 28.1 us  [per_device(): summed = jnp.sum(lax.all_gather(flat, ('gx', 'gy')), axis=0)]
    reduce_sum x1, other arithmetic: 0.97 us -> 2.61 us  [per_device(): summed = jnp.sum(lax.all_gather(flat, ('gx', 'gy')), axis=0)]
    reshape x1 -> x0, local copies, waits for them, and re-layouts: 1.15 us -> none  [per_device(): flat = partial_value.reshape(-1)]
where the time goes in v1:
time: 70.5 us; the launch traced here: 70.2 us
  waiting for transfers between devices  28.1 us (40%)
  between operations  18 us (26%)
  blocking collectives  12.3 us (17%)
  matrix products  5.86 us (8%)
  other arithmetic  4.26 us (6%)
  local copies, waits for them, and re-layouts  1.73 us (2%)
    all_gather x1, waiting for transfers between devices, per_device(): summed = jnp.sum(lax.all_gather(flat, ('gx', 'gy')), axis=0)  28.1 us
    psum x1, blocking collectives, settle(): gap, model = lax.psum((gap, model), 'var')  12.3 us
    reduce_sum x1, other arithmetic, per_device(): summed = jnp.sum(lax.all_gather(flat, ('gx', 'gy')), axis=0)  2.61 us
    dot_general x1, matrix products, per_device(): increment = jnp.einsum('lmj,im->lij', back, table_x, precision=high)  2.16 us
    dot_general x1, matrix products, per_device(): half = jnp.einsum('lij,im->lmj', block, table_x, precision=high)  2 us
  transfers between devices with their start and end apart: 1, of which 1 were waited for; matrix products, arithmetic and copies ran while one was open for 1% of the time, Pallas kernels for 0%

profile of v1, /device:TPU:0, one launch (start us, length us, event | category | flops | bytes accessed | tf_op | source)
XLA Modules:
  0.0 70.2 jit_solution(18307409709534928863)
XLA Ops:
  6.5 0.0 copy-start
  6.5 0.0 all-gather.3.cloned.1.call-start
  6.6 0.0 copy-start.5
  6.6 2.0 %convolution_bitcast_fusion = f32[32,40,128]{2,1,0:T(8,128)S(1)} fusion(f32[1,32,64,128]{3,2,1,0:T(8,128)} %param.6, f32[40]{0:T(128)S(1)} %compare_select_fusion.2, s32[64]{0:T(128)S(1)} %multiply_add_fusion.1), kind=kOutput, calls=%fused_computation.5 | convolution fusion | flops 125867520 | bytes 1704352 | tf_op jit(solution)/shard_map/lij,im->lmj/dot_general | solution.py:57
  8.6 0.7 %convolution_multiply_fusion.1 = f32[32,40,40]{2,1,0:T(8,128)S(1)} fusion(f32[32,40,128]{2,1,0:T(8,128)S(1)} %convolution_bitcast_fusion, f32[40]{0:T(128)S(1)} %compare_select_fusion.2, s32[128]{0:T(128)S(1)} %multiply_add_fusion), kind=kOutput, calls=%fused_computation.4 | convolution fusion | flops 78771200 | bytes 860832 | tf_op jit(solution)/shard_map/lmj,jn->lmn/dot_general | solution.py:58
  9.3 1.2 %reshape.47 = f32[1,1,51200]{2,1,0:T(1,128)} reshape(f32[32,40,40]{2,1,0:T(8,128)S(1)} %convolution_multiply_fusion.1) | data formatting | bytes 409600
  10.6 0.0 copy-start.2
  10.6 0.0 copy-start.3
  10.6 0.0 all-gather.3.cloned.1.call-update
  10.6 0.0 copy-done.5
  10.6 0.6 fusion.54
  11.2 28.1 %all-gather.3.cloned.1.call-done = f32[8,1,51200]{2,1,0:T(1,128)} async-done(((f32[1,1,51200]{2,1,0:T(1,128)}), f32[8,1,51200]{2,1,0:T(1,128)}) %all-gather.3.cloned.1.call-update) | async-done | bytes 1638416 | tf_op jit(solution)/shard_map/all_gather | solution.py:62
  39.3 2.6 %reduce_sum.37 = f32[51200]{0:T(1024)S(1)} reduce(f32[8,1,51200]{2,1,0:T(1,128)} %all-gather.3.cloned.1.call-done, f32[]{:T(128)} %constant.30.clone.1), dimensions={0,1}, to_apply=%region_1.2 | reduce | flops 358400 | bytes 1843204 | tf_op jit(solution)/shard_map/reduce_sum | solution.py:62
  42.0 0.5 reshape.46
  42.4 0.0 copy-done.2
  42.4 0.0 copy-done.3
  42.4 0.0 copy-start.4
  42.4 0.0 copy-start.1
  42.5 1.1 %fusion.5 = (f32[]{:T(128)}, f32[]{:T(128)}) fusion(f32[32,40,40]{2,1,0:T(8,128)S(1)} %reshape.46, s32[40,40]{1,0:T(8,128)S(1)} %iota_add_fusion, s32[32]{0:T(128)S(1)} %copy-done.3, f32[1,32,40,40]{3,2,1,0:T(8,128)S(1)} %copy-done.2), kind=kLoop, calls=%fused_computation.11 | loop fusion | flops 409598 | bytes 416136 | tf_op jit(solution)/shard_map/reduce_sum | solution.py:27
  45.9 0.8 %fusion.6 = f32[32,40,128]{2,1,0:T(8,128)S(1)} fusion(f32[32,40,40]{2,1,0:T(8,128)S(1)} %reshape.46, f32[1,32,40,40]{3,2,1,0:T(8,128)S(1)} %copy-done.2, s32[40,40]{1,0:T(8,128)S(1)} %iota_add_fusion, s32[32]{0:T(128)S(1)} %copy-done.3, f32[40]{0:T(128)S(1)} %compare_select_fusion.2, s32[128]{0:T(128)S(1)} %multiply_add_fusion), kind=kOutput, calls=%fused_computation.14 | convolution fusion | flops 78873600 | bytes 1072160 | tf_op jit(solution)/shard_map/lmn,jn->lmj/dot_general | solution.py:65
  46.7 12.3 %all-reduce = (f32[]{:T(128)}, f32[]{:T(128)}) all-reduce(f32[]{:T(128)S(6)} %mul.132, f32[]{:T(128)S(6)} %mul.135), channel_id=1, replica_groups=mesh['gx'=4,'gy'=2,'var'=4] {'var'}, use_global_device_ids=true, to_apply=%region_3.4 | all-reduce | flops 2 | bytes 16 | tf_op jit(solution)/shard_map/psum | solution.py:28
  61.0 0.0 copy-done
  61.0 0.0 copy-done.4
  61.0 0.2 fusion.3
  61.2 0.0 copy-done.1
  61.2 2.2 %fusion.2 = f32[1,32,64,128]{3,2,1,0:T(8,128)} fusion(f32[32,40,128]{2,1,0:T(8,128)S(1)} %fusion.6, f32[1,32,64,128]{3,2,1,0:T(8,128)S(1)} %copy-done.1, f32[32]{0:T(128)S(1)} %fusion.3, f32[40]{0:T(128)S(1)} %compare_select_fusion.2, s32[64]{0:T(128)S(1)} %multiply_add_fusion.1), kind=kOutput, calls=%fused_computation.3 | convolution fusion | flops 126391808 | bytes 2753056 | tf_op jit(solution)/shard_map/lmj,im->lij/dot_general | solution.py:66
  (4 shorter events, 0.0 us)
Async XLA Ops:
  6.5 54.5 %copy-start = (f32[8]{0:T(128)S(1)}, f32[8]{0:T(128)}, u32[]{:S(2)}) copy-start(f32[8]{0:T(128)} %param.10) | copy-start | bytes 100
  6.5 32.8 %all-gather.3.cloned.1.call-start = ((), (), s32[]{:S(2)}) async-start(), calls=%async_computation | async-start | bytes 1843200 | tf_op jit(solution)/shard_map/all_gather | solution.py:62
  6.6 4.1 %copy-start.5 = (f32[4]{0:T(128)S(1)}, f32[4]{0:T(128)}, u32[]{:S(2)}) copy-start(f32[4]{0:T(128)} %constant.72.clone) | copy-start | bytes 52
  10.6 31.8 %copy-start.2 = (f32[1,32,40,40]{3,2,1,0:T(8,128)S(1)}, f32[1,32,40,40]{3,2,1,0:T(8,128)}, u32[]{:S(2)}) copy-start(f32[1,32,40,40]{3,2,1,0:T(8,128)} %param.7) | copy-start | bytes 614404
  10.6 31.8 %copy-start.3 = (s32[32]{0:T(128)S(1)}, s32[32]{0:T(128)}, u32[]{:S(2)}) copy-start(s32[32]{0:T(128)} %param.8) | copy-start | bytes 388
  42.4 18.6 %copy-start.4 = (s32[32]{0:T(128)S(1)}, s32[32]{0:T(128)}, u32[]{:S(2)}) copy-start(s32[32]{0:T(128)} %param.9) | copy-start | bytes 388
  42.4 18.8 %copy-start.1 = (f32[1,32,64,128]{3,2,1,0:T(8,128)S(1)}, f32[1,32,64,128]{3,2,1,0:T(8,128)}, u32[]{:S(2)}) copy-start(f32[1,32,64,128]{3,2,1,0:T(8,128)} %param.6) | copy-start | bytes 3145732
Sparse Core Ops, SparseCore 0:
  10.7 28.5 all-gather.2
